TPU v7x, 128 devices: a whole 4x4x4 slice. The times are simulated.
128 devices in a mesh: dp: 1, vp: 128 (over z, y, x, core).
Axes of the slice: x: 4, y: 4, z: 4, core: 2. Of those that a mesh axis runs over, the one named last changes fastest.
Arguments:
- hidden: bfloat16 [256, 32, 640], P('vp', 'dp')
- norm_gain: float32 [640], replicated
- norm_bias: float32 [640], replicated
- w_out: bfloat16 [640, 262144], P(None, 'vp')
- labels: int32 [256, 32], P('vp', 'dp')
- loss_mask: float32 [256, 32], P('vp', 'dp')
Outputs:
- output 1: float32 [1], P('dp')
- output 2: bfloat16 [256, 32, 640], P('vp', 'dp')
- output 3: float32 [640, 262144], P('dp', 'vp')
- output 4: float32 [640], P('dp')
- output 5: float32 [640], P('dp')
All inputs are finite; a program needn't handle non-finite values.
Results may differ from a plain program's by a relative error of at most 0.001.
Values are sent between devices in bfloat16 or wider.
A program may use at most 1 GiB of HBM per device.

v0:
```python
import jax
import jax.numpy as jnp
from jax import lax
from jax.sharding import PartitionSpec as P

NORM_EPS = 1e-5


def norm_forward(hidden, norm_gain, norm_bias):
    x_float = hidden.astype(jnp.float32)
    tok_mean = jnp.mean(x_float, axis=-1, keepdims=True)
    centered = x_float - tok_mean
    inv_std = lax.rsqrt(jnp.mean(centered * centered, axis=-1, keepdims=True) + NORM_EPS)
    normed = centered * inv_std
    h_bf = (normed * (1.0 + norm_gain) + norm_bias).astype(jnp.bfloat16)
    return h_bf, normed, inv_std


def norm_backward(grad_h, normed, inv_std, norm_gain):
    scaled = grad_h * (1.0 + norm_gain)
    centered_grad = scaled - jnp.mean(scaled, axis=-1, keepdims=True)
    return (inv_std * (centered_grad - normed * jnp.mean(scaled * normed, axis=-1, keepdims=True))).astype(jnp.bfloat16)


def solution(mesh):
    def per_device(hidden, norm_gain, norm_bias, w_blk, labels, loss_mask):
        h_bf, normed, inv_std = norm_forward(hidden, norm_gain, norm_bias)
        h_all = lax.all_gather(h_bf, "vp", axis=0, tiled=True)
        labels_all = lax.all_gather(labels, "vp", axis=0, tiled=True)
        mask_all = lax.all_gather(loss_mask, "vp", axis=0, tiled=True)
        vocab_local = w_blk.shape[1]
        col_start = lax.axis_index("vp") * vocab_local
        logits = jnp.einsum("sbd,dv->sbv", h_all, w_blk, preferred_element_type=jnp.float32)
        row_max = lax.pmax(jnp.max(logits, axis=-1), "vp")
        exp_shift = jnp.exp(logits - row_max[:, :, None])
        col_ids = col_start + lax.broadcasted_iota(jnp.int32, (1, 1, vocab_local), 2)
        is_label = col_ids == labels_all[:, :, None]
        sum_exp = lax.psum(jnp.sum(exp_shift, axis=-1), "vp")
        target = lax.psum(jnp.sum(jnp.where(is_label, logits, 0.0), axis=-1), "vp")
        mask_total = jnp.sum(mask_all)
        tok_loss = row_max + jnp.log(sum_exp) - target
        loss = jnp.sum(mask_all * tok_loss) / mask_total
        prob_soft = exp_shift / sum_exp[:, :, None]
        tok_weight = mask_all / mask_total
        grad_logits = (jnp.where(is_label, prob_soft - 1.0, prob_soft) * tok_weight[:, :, None]).astype(jnp.bfloat16)
        grad_w = jnp.einsum("sbd,sbv->dv", h_all, grad_logits, preferred_element_type=jnp.float32)
        grad_h_part = jnp.einsum("sbv,dv->sbd", grad_logits, w_blk, preferred_element_type=jnp.float32)
        grad_h = lax.psum_scatter(grad_h_part, "vp", scatter_dimension=0, tiled=True)
        grad_gain = lax.psum(jnp.sum(grad_h * normed, axis=(0, 1)), "vp")
        grad_bias = lax.psum(jnp.sum(grad_h, axis=(0, 1)), "vp")
        grad_x = norm_backward(grad_h, normed, inv_std, norm_gain)
        return loss.reshape(1), grad_x, grad_w, grad_gain, grad_bias

    tok_spec = P("vp", "dp")
    return jax.shard_map(
        per_device,
        mesh=mesh,
        in_specs=(P("vp", "dp", None), P(None), P(None), P(None, "vp"), tok_spec, tok_spec),
        out_specs=(P("dp"), P("vp", "dp", None), P("dp", "vp"), P("dp"), P("dp")),
        check_vma=False,
    )
```

profile of v0, /device:TPU:0, one launch (start us, length us, event | category | flops | bytes accessed | tf_op | source)
XLA Modules:
  0.0 1111.7 jit_solution(10096994293831774632)
XLA Ops:
  7.2 0.0 copy-start
  7.2 0.0 all-gather.4.cloned.1.call-start
  7.2 1.1 convert_reduce_fusion
  8.4 0.0 copy-start.6
  8.4 1.1 fusion.28
  9.4 0.0 copy-start.8
  9.5 0.7 broadcast_add_fusion
  10.1 0.0 copy-done.6
  10.1 0.0 copy-done.8
  10.2 0.0 copy-start.4
  10.2 0.6 copy-done.4
  10.7 1.6 fusion.22
  12.4 0.0 all-gather.4.cloned.1.call-update
  12.4 0.0 reduce-scatter.2.cloned.1.call-start
  12.4 37.7 %all-gather = f32[128,2,32]{2,1,0:T(2,128)S(1)} all-gather(f32[1,2,32]{2,1,0:T(2,128)} %bitcast.17), channel_id=1, replica_groups=mesh['dp'=1,'vp'=128] {'vp'}, dimensions={0}, use_global_device_ids=true | all-gather | bytes 33024 | tf_op jit(solution)/shard_map/all_gather | solution.py:30
  50.2 0.7 reduce_sum.95
  50.9 0.1 copy.18
  51.0 0.0 copy-start.2
  51.0 33.8 %all-gather.1 = s32[128,2,32]{2,1,0:T(2,128)S(1)} all-gather(s32[1,2,32]{2,1,0:T(2,128)} %bitcast.18), channel_id=1, replica_groups=mesh['dp'=1,'vp'=128] {'vp'}, dimensions={0}, use_global_device_ids=true | all-gather | bytes 33024 | tf_op jit(solution)/shard_map/all_gather | solution.py:29
  84.8 0.1 copy.17
  84.8 0.7 broadcast_divide_fusion
  85.5 0.7 all-gather.4.cloned.1.call-done
  86.2 0.0 copy-done
  86.2 35.5 %fusion.29 = (f32[256,32]{0,1:T(8,128)S(1)}, f32[256,32,2048]{2,0,1:T(8,128)}) fusion(bf16[640,2048]{1,0:T(8,128)(2,1)S(1)} %copy-done, bf16[256,32,640]{2,1,0:T(8,128)(2,1)} %all-gather.4.cloned.1.call-done), kind=kOutput, calls=%fused_computation.41 | convolution fusion | flops 21491605504 | bytes 80248832 | tf_op jit(solution)/shard_map/sbd,dv->sbv/dot_general | solution.py:33
  121.7 0.0 copy-done.2
  121.7 64.2 %pmax.7 = f32[256,32]{0,1:T(8,128)S(1)} all-reduce(f32[256,32]{0,1:T(8,128)S(1)} %get-tuple-element.19), channel_id=1, replica_groups=mesh['dp'=1,'vp'=128] {'vp'}, use_global_device_ids=true, to_apply=%region_3.0 | all-reduce | flops 8192 | bytes 65536 | tf_op jit(solution)/shard_map/pmax | solution.py:34
  185.9 21.5 %fusion.3 = (f32[256,32]{0,1:T(8,128)S(1)}, f32[256,32]{0,1:T(8,128)S(1)}) fusion(f32[256,32,2048]{2,0,1:T(8,128)} %get-tuple-element.20, f32[256,32]{0,1:T(8,128)S(1)} %pmax.7, s32[256,32]{0,1:T(8,128)S(1)} %copy.17, s32[2048]{0:T(1024)S(1)} %iota_add_fusion), kind=kLoop, calls=%fused_computation.6 | loop fusion | flops 83869696 | bytes 67248128 | tf_op jit(solution)/shard_map/reduce_sum | solution.py:38
  207.4 64.3 %psum.28 = f32[256,32]{0,1:T(8,128)S(1)} all-reduce(f32[256,32]{0,1:T(8,128)S(1)} %get-tuple-element.10), channel_id=1, replica_groups=mesh['dp'=1,'vp'=128] {'vp'}, use_global_device_ids=true, to_apply=%region_5.0 | all-reduce | flops 8192 | bytes 65536 | tf_op jit(solution)/shard_map/psum | solution.py:38
  271.7 33.7 %fusion.2 = bf16[256,32,2048]{2,0,1:T(8,128)(2,1)} fusion(f32[256,32,2048]{2,0,1:T(8,128)} %get-tuple-element.20, f32[256,32]{0,1:T(8,128)S(1)} %broadcast_divide_fusion, f32[256,32]{0,1:T(8,128)S(1)} %psum.28, s32[256,32]{0,1:T(8,128)S(1)} %copy.17, s32[2048]{0:T(1024)S(1)} %iota_add_fusion, f32[256,32]{0,1:T(8,128)S(1)} %pmax.7), kind=kLoop, calls=%fused_computation.4 | loop fusion | flops 117440512 | bytes 100802560 | tf_op jit(solution)/shard_map/convert_element_type | solution.py:45
  305.4 55.4 %fusion.6 = f32[256,32,640]{2,1,0:T(8,128)} fusion(bf16[256,32,2048]{2,0,1:T(8,128)(2,1)} %fusion.2, bf16[640,2048]{1,0:T(8,128)(2,1)S(1)} %copy-done), kind=kOutput, calls=%fused_computation.9 | convolution fusion | flops 21474836480 | bytes 57147392 | tf_op jit(solution)/shard_map/sbv,dv->sbd/dot_general | solution.py:47
  360.8 0.0 reduce-scatter.2.cloned.1.call-update
  360.8 0.0 copy-start.1
  360.8 0.0 copy-start.5
  360.8 0.0 copy-start.7
  360.9 0.0 copy-start.9
  360.9 0.0 copy-start.3
  360.9 42.2 %fusion.10 = f32[640,2048]{1,0:T(8,128)} fusion(bf16[256,32,640]{2,1,0:T(8,128)(2,1)} %all-gather.4.cloned.1.call-done, bf16[256,32,2048]{2,0,1:T(8,128)(2,1)} %fusion.2), kind=kOutput, calls=%fused_computation.13 | convolution fusion | flops 21474836480 | bytes 49283072 | tf_op jit(solution)/shard_map/sbd,sbv->dv/dot_general | solution.py:46
  403.0 633.1 %reduce-scatter.2.cloned.1.call-done = f32[2,32,640]{2,1,0:T(8,128)} async-done(((f32[256,32,640]{2,1,0:T(8,128)}), f32[2,32,640]{2,1,0:T(8,128)}) %reduce-scatter.2.cloned.1.call-update) | async-done | bytes 163856 | tf_op jit(solution)/shard_map/reduce_scatter | solution.py:48
  1036.2 0.0 copy-done.1
  1036.2 0.0 copy-done.5
  1036.2 0.0 copy-done.7
  1036.2 0.0 copy-done.9
  1036.2 1.1 fusion.27
  1037.3 62.8 %all-reduce = (f32[256,32]{0,1:T(8,128)S(1)}, f32[640]{0:T(1024)}, f32[640]{0:T(1024)}) all-reduce(f32[256,32]{0,1:T(8,128)S(1)} %get-tuple-element.11, f32[640]{0:T(1024)S(1)} %get-tuple-element.12, f32[640]{0:T(1024)S(1)} %get-tuple-element.15), channel_id=1, replica_groups=mesh['dp'=1,'vp'=128] {'vp'}, use_global_device_ids=true, to_apply=%region_7.8 | all-reduce | flops 9472 | bytes 75776 | tf_op jit(solution)/shard_map/psum | solution.py:39
  1100.1 0.0 copy-done.3
  1100.1 0.6 multiply_reduce_fusion.1
  1102.1 1.7 fusion.26
  (4 shorter events, 0.0 us)
Async XLA Ops:
  7.2 79.0 %copy-start = (bf16[640,2048]{1,0:T(8,128)(2,1)S(1)}, bf16[640,2048]{1,0:T(8,128)(2,1)}, u32[]{:S(2)}) copy-start(bf16[640,2048]{1,0:T(8,128)(2,1)} %param.9) | copy-start | bytes 7864324
  7.2 79.0 %all-gather.4.cloned.1.call-start = ((), (), s32[]{:S(2)}) async-start(), calls=%async_computation.1 | async-start | bytes 10567680 | tf_op jit(solution)/shard_map/all_gather | solution.py:28
  8.4 1.8 copy-start.6
  9.4 0.7 copy-start.8
  10.2 0.6 copy-start.4
  12.4 1023.8 %reduce-scatter.2.cloned.1.call-start = ((), (), s32[]{:S(2)}) async-start(), calls=%async_computation.2 | async-start | bytes 21135360 | tf_op jit(solution)/shard_map/reduce_scatter | solution.py:48
  51.0 70.7 %copy-start.2 = (f32[256,32]{0,1:T(8,128)}, f32[256,32]{0,1:T(8,128)S(1)}, u32[]{:S(2)}) copy-start(f32[256,32]{0,1:T(8,128)S(1)} %copy.18) | copy-start | bytes 98308
  360.8 675.3 %copy-start.1 = (bf16[2,32,640]{2,1,0:T(8,128)(2,1)S(1)}, bf16[2,32,640]{2,1,0:T(8,128)(2,1)}, u32[]{:S(2)}) copy-start(bf16[2,32,640]{2,1,0:T(8,128)(2,1)} %param.6) | copy-start | bytes 245764
  360.8 675.3 %copy-start.5 = (f32[640]{0:T(1024)S(1)}, f32[640]{0:T(1024)}, u32[]{:S(2)}) copy-start(f32[640]{0:T(1024)} %copy-done.4) | copy-start | bytes 7684
  360.8 675.3 %copy-start.7 = (f32[2,32]{1,0:T(2,128)S(1)}, f32[2,32]{1,0:T(2,128)}, u32[]{:S(2)}) copy-start(f32[2,32]{1,0:T(2,128)} %copy-done.6) | copy-start | bytes 772
  360.9 675.3 %copy-start.9 = (f32[2,32]{1,0:T(2,128)S(1)}, f32[2,32]{1,0:T(2,128)}, u32[]{:S(2)}) copy-start(f32[2,32]{1,0:T(2,128)} %copy-done.8) | copy-start | bytes 772
  360.9 739.3 %copy-start.3 = (f32[256,32]{0,1:T(8,128)S(1)}, f32[256,32]{0,1:T(8,128)}, u32[]{:S(2)}) copy-start(f32[256,32]{0,1:T(8,128)} %copy-done.2) | copy-start | bytes 98308
Sparse Core Ops, SparseCore 0:
  12.5 73.6 all-gather.3
  360.9 675.1 reduce-scatter.1
where the time goes:
time: 1110 us
  waiting for transfers between devices  634 us (57%)
  blocking collectives  263 us (24%)
  matrix products  133 us (12%)
  other arithmetic  64.5 us (6%)
  between operations  16.6 us (1%)
    reduce_scatter x1, waiting for transfers between devices, per_device(): lax.psum_scatter(grad_h_part, 'vp', scatter_dimension=0, tiled=True)  633 us
    psum x1, blocking collectives, per_device(): sum_exp = lax.psum(jnp.sum(exp_shift, axis=-1), 'vp')  64.3 us
    pmax x1, blocking collectives, per_device(): row_max = lax.pmax(jnp.max(logits, axis=-1), 'vp')  64.2 us
    psum x1, blocking collectives, per_device(): target = lax.psum(jnp.sum(jnp.where(is_label, logits, 0.0), axis=-1), 'vp')  62.8 us
    dot_general x1, matrix products, per_device(): jnp.einsum('sbv,dv->sbd', grad_logits, w_blk, preferred_element_type=jnp....  55.4 us
    dot_general x1, matrix products, per_device(): jnp.einsum('sbd,sbv->dv', h_all, grad_logits, preferred_element_type=jnp....  42.2 us
    all_gather x1, blocking collectives, per_device(): mask_all = lax.all_gather(loss_mask, 'vp', axis=0, tiled=True)  37.7 us
    dot_general x1, matrix products, per_device(): jnp.einsum('sbd,dv->sbv', h_all, w_blk, preferred_element_type=jnp.float32)  35.5 us
  transfers between devices with their start and end apart: 2, of which 2 were waited for; matrix products, arithmetic and copies ran while one was open for 4% of the time, Pallas kernels for 0%

commit v1 on v0

v1 whole, which is shorter than its diff:
```python
import jax
import jax.numpy as jnp
from jax import lax
from jax.experimental import pallas as pl
from jax.experimental.pallas import tpu as pltpu
from jax.sharding import PartitionSpec as P

NORM_EPS = 1e-5
F32 = jnp.float32
BF16 = jnp.bfloat16
SIDE = 4
ORDERS = (("x", "y", "z"), ("y", "z", "x"), ("z", "x", "y"))
AXPOS = {"z": 0, "y": 1, "x": 2}
TOK = 64
DM = 640
VL = 2048
NTOK = 4096
TB = 512
NB = NTOK // TB
CT = 1024
VMEM_CAP = 64 * 1024 * 1024 - 65536


def here():
    me = lax.axis_index("vp")
    chip = me // 2
    return {"core": me % 2, "x": chip % SIDE, "y": (chip // SIDE) % SIDE, "z": chip // (SIDE * SIDE)}


def dev_of(pos):
    return ((pos["z"] * SIDE + pos["y"]) * SIDE + pos["x"]) * 2 + pos["core"]


def shifted(pos, axis, delta):
    out = dict(pos)
    if axis == "core":
        out["core"] = 1 - pos["core"]
    else:
        out[axis] = (pos[axis] + delta + SIDE) % SIDE
    return {"vp": dev_of(out)}


def barrier_with(peers):
    sem = pltpu.get_barrier_semaphore()
    for peer in peers:
        pl.semaphore_signal(sem, inc=1, device_id=peer, device_id_type=pl.DeviceIdType.MESH)
    pl.semaphore_wait(sem, len(peers))


def ring_peers(pos, deltas):
    return [shifted(pos, ax, d) for ax in ("x", "y", "z") for d in deltas] + [shifted(pos, "core", 0)]


def rcopy(src, dst, ssem, rsem, peer):
    return pltpu.make_async_remote_copy(src_ref=src, dst_ref=dst, send_sem=ssem, recv_sem=rsem,
                                        device_id=peer, device_id_type=pl.DeviceIdType.MESH)


def gather_kernel(h0, h1, h2, w_in, g0, g1, g2, w_oth, ssem, rsem, lsem, wsem):
    pos = here()
    barrier_with(ring_peers(pos, (1, -1)))
    wcopy = rcopy(w_in, w_oth, wsem.at[0], wsem.at[1], shifted(pos, "core", 0))
    wcopy.start()
    hs, gs = (h0, h1, h2), (g0, g1, g2)
    local = []
    for c in range(3):
        cp = pltpu.make_async_copy(hs[c], gs[c].at[pos["z"], pos["y"], pos["x"]], lsem.at[c])
        cp.start()
        local.append(cp)

    def unit(c, phase, coord):
        axis = ORDERS[c][phase]
        done = ORDERS[c][:phase]
        idx = []
        for ax in ("z", "y", "x"):
            if ax in done:
                idx.append(slice(None))
            elif ax == axis:
                idx.append(coord)
            else:
                idx.append(pos[ax])
        return tuple(idx)

    sends = []
    for phase in range(3):
        first = {}
        for c in range(3):
            axis = ORDERS[c][phase]
            me = pos[axis]
            if phase == 1:
                local[c].wait()
            for k, d in ((0, 1), (1, -1)):
                slot = (c * 3 + phase) * 4 + k
                own = gs[c].at[unit(c, phase, me)]
                src = hs[c] if phase == 0 else own
                cp = rcopy(src, own, ssem.at[slot], rsem.at[slot], shifted(pos, axis, d))
                cp.start()
                sends.append(cp)
                first[c, k] = cp
        second = []
        for c in range(3):
            axis = ORDERS[c][phase]
            me = pos[axis]
            for k, d in ((0, 1), (1, -1)):
                slot = (c * 3 + phase) * 4 + 2 + k
                first[c, k].wait_recv()
                blk = gs[c].at[unit(c, phase, (me - d + SIDE) % SIDE)]
                half = blk.at[(slice(None),) * (phase + 1) + (pl.ds(128 * k, 128),)]
                cp = rcopy(half, half, ssem.at[slot], rsem.at[slot], shifted(pos, axis, d))
                cp.start()
                sends.append(cp)
                second.append(cp)
        for cp in second:
            cp.wait_recv()
    for cp in sends:
        cp.wait_send()
    wcopy.wait()


def gather_call(h0, h1, h2, w_blk):
    vm = pl.BlockSpec(memory_space=pltpu.VMEM)
    anyspec = pl.BlockSpec(memory_space=pl.ANY)
    gshape = jax.ShapeDtypeStruct((SIDE, SIDE, SIDE, TOK, 256), BF16)
    return pl.pallas_call(
        gather_kernel,
        out_shape=(gshape, gshape, gshape, jax.ShapeDtypeStruct((DM, VL), BF16)),
        in_specs=[vm, vm, vm, anyspec],
        out_specs=(vm, vm, vm, anyspec),
        scratch_shapes=[pltpu.SemaphoreType.DMA((36,)), pltpu.SemaphoreType.DMA((36,)),
                        pltpu.SemaphoreType.DMA((3,)), pltpu.SemaphoreType.DMA((2,))],
        compiler_params=pltpu.CompilerParams(collective_id=1, has_side_effects=True, vmem_limit_bytes=VMEM_CAP),
    )(h0, h1, h2, w_blk)


def label_minus_lane(aux):
    lab = aux[:, 0:1] + aux[:, 1:2] * 256.0 + aux[:, 2:3] * 65536.0
    lane = lax.broadcasted_iota(jnp.int32, (aux.shape[0], 128), 1)
    return lab.astype(jnp.int32) - lane


def logits_kernel(g0, g1, g2, w_own, w_oth, z_own, z_oth, lse_out, mt_out, ms_out,
                  zA, zB, m_s, s_s, t_s, lab_s, sem):
    pos = here()
    base_own = dev_of(pos) * VL
    base_oth = dev_of({**pos, "core": 1 - pos["core"]}) * VL
    zbuf = (zA, zB)
    tiles = ((w_own, z_own, 0, base_own), (w_own, z_own, CT, base_own), (w_oth, z_oth, 0, base_oth), (w_oth, z_oth, CT, base_oth))
    mt_out[...] = jnp.zeros_like(mt_out)
    ms_out[...] = jnp.zeros_like(ms_out)

    def stats(buf, cbase, first, rows):
        zt = buf[rows, :]
        tile_max = zt[:, 0:128]
        for k in range(1, CT // 128):
            tile_max = jnp.maximum(tile_max, zt[:, 128 * k:128 * k + 128])
        labm = lab_s[rows, :]
        if first:
            m_new = tile_max
        else:
            m_old = m_s[rows, :]
            m_new = jnp.maximum(m_old, tile_max)
        acc = None
        tacc = None
        for k in range(CT // 128):
            zk = zt[:, 128 * k:128 * k + 128]
            e = jnp.exp(zk - m_new)
            hit = jnp.where(labm == cbase + 128 * k, zk, 0.0)
            acc = e if acc is None else acc + e
            tacc = hit if tacc is None else tacc + hit
        if first:
            s_s[rows, :] = acc
            t_s[rows, :] = tacc
        else:
            s_s[rows, :] = s_s[rows, :] * jnp.exp(m_old - m_new) + acc
            t_s[rows, :] = t_s[rows, :] + tacc
        m_s[rows, :] = m_new

    def block(i, carry):
        tok = pl.ds(pl.multiple_of(i * TB, TB), TB)
        a0 = g0[tok, :]
        a1 = g1[tok, :]
        a2 = g2[tok, 0:128]
        aux = g2[tok, 128:256].astype(F32)
        lab_s[...] = label_minus_lane(aux)
        for seg in range(5):
            if seg < 4:
                w_ref, z_ref, off, _ = tiles[seg]
                buf = zbuf[seg % 2]
                out = pltpu.make_async_copy(buf, z_ref.at[tok, pl.ds(off, CT)], sem.at[seg % 2])
                if seg >= 2:
                    out.wait()
                else:
                    @pl.when(i > 0)
                    def _():
                        out.wait()
            for sub in range(4):
                if seg < 4:
                    cols = pl.ds(off + 256 * sub, 256)
                    zt = jnp.dot(a0, w_ref[0:256, cols], preferred_element_type=F32)
                    zt += jnp.dot(a1, w_ref[256:512, cols], preferred_element_type=F32)
                    zt += jnp.dot(a2, w_ref[512:640, cols], preferred_element_type=F32)
                    buf[:, 256 * sub:256 * sub + 256] = zt
                if seg > 0:
                    _, _, poff, pbase = tiles[seg - 1]
                    for r in range(8):
                        stats(zbuf[(seg - 1) % 2], pbase + poff, seg == 1, pl.ds(sub * 128 + r * 16, 16))
            if seg < 4:
                out.start()
        mt = m_s[...].T
        st = s_s[...].T
        mx = jnp.max(mt, axis=0, keepdims=True)
        tot = jnp.sum(st * jnp.exp(mt - mx), axis=0, keepdims=True)
        lse_out[pl.ds(i, 1), :] = mx + jnp.log(tot)
        mcol = aux[:, 3:4]
        mt_out[...] += jnp.sum((t_s[...] * mcol).reshape(TB // 8, 8, 128), axis=0)
        ms_out[...] += jnp.sum(jnp.broadcast_to(mcol, (TB, 128)).reshape(TB // 8, 8, 128), axis=0)
        return carry

    lax.fori_loop(0, NB, block, 0)
    for k in range(2):
        pltpu.make_async_copy(zbuf[k], z_oth.at[pl.ds(0, TB), pl.ds(0, CT)], sem.at[k]).wait()


def logits_call(g0, g1, g2, w_own, w_oth):
    vm = pl.BlockSpec(memory_space=pltpu.VMEM)
    anyspec = pl.BlockSpec(memory_space=pl.ANY)
    zshape = jax.ShapeDtypeStruct((NTOK, VL), F32)
    return pl.pallas_call(
        logits_kernel,
        out_shape=(zshape, zshape, jax.ShapeDtypeStruct((NB, TB), F32), jax.ShapeDtypeStruct((8, 128), F32), jax.ShapeDtypeStruct((8, 128), F32)),
        in_specs=[vm] * 5,
        out_specs=(anyspec, anyspec, vm, vm, vm),
        scratch_shapes=[pltpu.VMEM((TB, CT), F32), pltpu.VMEM((TB, CT), F32)] + [pltpu.VMEM((TB, 128), F32)] * 3
        + [pltpu.VMEM((TB, 128), jnp.int32), pltpu.SemaphoreType.DMA((2,))],
        compiler_params=pltpu.CompilerParams(vmem_limit_bytes=VMEM_CAP),
    )(g0, g1, g2, w_own, w_oth)


def lse_kernel(lse_in, ms_in, lse_out, ms_out, cur, got, mgot, ssem, rsem):
    pos = here()
    barrier_with(ring_peers(pos, (1, 2, 3)))
    mcopy = rcopy(ms_in, mgot, ssem.at[9], rsem.at[9], shifted(pos, "core", 0))
    mcopy.start()
    for p, axis in enumerate(("x", "y", "z")):
        src = lse_in if p == 0 else cur.at[p - 1]
        cps = []
        for d in (2, 1, 3):
            k = p * 3 + d - 1
            cp = rcopy(src, got.at[k], ssem.at[k], rsem.at[k], shifted(pos, axis, d))
            cp.start()
            cps.append(cp)
        for cp in cps:
            cp.wait()
        v = [src[...], got[p * 3], got[p * 3 + 1], got[p * 3 + 2]]
        mx = jnp.maximum(jnp.maximum(v[0], v[1]), jnp.maximum(v[2], v[3]))
        tot = (jnp.exp(v[0] - mx) + jnp.exp(v[1] - mx)) + (jnp.exp(v[2] - mx) + jnp.exp(v[3] - mx))
        res = mx + jnp.log(tot)
        if p < 2:
            cur[p] = res
        else:
            lse_out[...] = res
    mcopy.wait()
    tot = jnp.sum(ms_in[...] + mgot[...], axis=0, keepdims=True)
    ms_out[...] = jnp.broadcast_to(tot, ms_out.shape)


def lse_call(lse_loc, msum):
    vm = pl.BlockSpec(memory_space=pltpu.VMEM)
    return pl.pallas_call(
        lse_kernel,
        out_shape=(jax.ShapeDtypeStruct((NB, TB), F32), jax.ShapeDtypeStruct((8, 128), F32)),
        in_specs=[vm, vm],
        out_specs=(vm, vm),
        scratch_shapes=[pltpu.VMEM((2, NB, TB), F32), pltpu.VMEM((9, NB, TB), F32), pltpu.VMEM((8, 128), F32),
                        pltpu.SemaphoreType.DMA((10,)), pltpu.SemaphoreType.DMA((10,))],
        compiler_params=pltpu.CompilerParams(collective_id=2, has_side_effects=True),
    )(lse_loc, msum)


def grads_kernel(g0, g1, g2, w_own, w_oth, z_own, z_oth, lse, msum, dh_out, dw_own, dw_oth,
                 zA, zB, dA, dB, hT, dh_s, lse_s, wt_s, lab_s, zsem, osem):
    pos = here()
    base_own = dev_of(pos) * VL
    base_oth = dev_of({**pos, "core": 1 - pos["core"]}) * VL
    zbuf, dbuf = (zA, zB), (dA, dB)
    tiles = ((w_own, z_own, 0, base_own, dw_own), (w_own, z_own, CT, base_own, dw_own),
             (w_oth, z_oth, 0, base_oth, dw_oth), (w_oth, z_oth, CT, base_oth, dw_oth))

    def zcopy(i, t):
        _, z_ref, off, _, _ = tiles[t]
        tok = pl.ds(pl.multiple_of(i * TB, TB), TB)
        return pltpu.make_async_copy(z_ref.at[tok, pl.ds(off, CT)], zbuf[t % 2], zsem.at[t % 2])

    def prep(i):
        tok = pl.ds(pl.multiple_of(i * TB, TB), TB)
        aux = g2[tok, 128:256].astype(F32)
        lab_s[...] = label_minus_lane(aux)
        wt_s[...] = jnp.broadcast_to(aux[:, 3:4], (TB, 128)) / msum[0:1, :]
        lse_s[...] = jnp.broadcast_to(lse[pl.ds(i, 1), :], (128, TB)).T

    def make_dz(t, r):
        _, _, off, base, _ = tiles[t]
        rows = pl.ds(r * 16, 16)
        lse_b = lse_s[rows, :]
        wt = wt_s[rows, :]
        labm = lab_s[rows, :]
        for k in range(CT // 128):
            ks = slice(128 * k, 128 * k + 128)
            p = jnp.exp(zbuf[t % 2][rows, ks] - lse_b)
            p = jnp.where(labm == base + off + 128 * k, p - 1.0, p)
            dbuf[t % 2][rows, ks] = (p * wt).astype(BF16)

    dw_own[...] = jnp.zeros_like(dw_own)
    dw_oth[...] = jnp.zeros_like(dw_oth)
    zcopy(0, 0).start()
    zcopy(0, 1).start()
    prep(0)
    zcopy(0, 0).wait()
    for r in range(TB // 16):
        make_dz(0, r)
    zcopy(0, 2).start()

    def block(i, carry):
        tok = pl.ds(pl.multiple_of(i * TB, TB), TB)
        hT[0:256, :] = g0[tok, :].T
        hT[256:512, :] = g1[tok, :].T
        hT[512:640, :] = g2[tok, 0:128].T
        for seg in range(4):
            w_ref, _, off, _, dw_ref = tiles[seg]
            dz = dbuf[seg % 2]
            nt = (seg + 1) % 4
            if seg == 3:
                nxt = jnp.minimum(i + 1, NB - 1)
                prep(nxt)
            else:
                nxt = i
            zcopy(nxt, nt).wait()
            piece = 0
            for n in range(3):
                lo, hi = 256 * n, min(256 * n + 256, DM)
                part = lax.dot_general(dz[...], w_ref[lo:hi, pl.ds(off, CT)], (((1,), (1,)), ((), ())), preferred_element_type=F32)
                if seg == 0:
                    dh_s[:, lo:hi] = part
                else:
                    dh_s[:, lo:hi] += part
                for r in range(4):
                    make_dz(nt, piece)
                    piece += 1
            for sub in range(4):
                cols = pl.ds(off + 256 * sub, 256)
                dw_ref[:, cols] += jnp.dot(hT[...], dz[:, 256 * sub:256 * sub + 256], preferred_element_type=F32)
                for r in range(5):
                    make_dz(nt, piece)
                    piece += 1
            after = jnp.minimum(i + (seg + 3) // 4, NB - 1)
            zcopy(after, (seg + 3) % 4).start()
        return carry

    def block_out(i, carry):
        block(i, carry)
        tok = pl.ds(pl.multiple_of(i * TB, TB), TB)
        cp = pltpu.make_async_copy(dh_s, dh_out.at[tok, :], osem.at[0])
        cp.start()
        cp.wait()
        return carry

    lax.fori_loop(0, NB, block_out, 0)
    zcopy(NB - 1, 1).wait()
    zcopy(NB - 1, 2).wait()


def grads_call(g0, g1, g2, w_own, w_oth, z_own, z_oth, lse, msum):
    vm = pl.BlockSpec(memory_space=pltpu.VMEM)
    anyspec = pl.BlockSpec(memory_space=pl.ANY)
    dwshape = jax.ShapeDtypeStruct((DM, VL), F32)
    return pl.pallas_call(
        grads_kernel,
        out_shape=(jax.ShapeDtypeStruct((NTOK, DM), F32), dwshape, dwshape),
        in_specs=[vm] * 5 + [anyspec] * 2 + [vm] * 2,
        out_specs=(anyspec, vm, vm),
        scratch_shapes=[pltpu.VMEM((TB, CT), F32)] * 2 + [pltpu.VMEM((TB, CT), BF16)] * 2
        + [pltpu.VMEM((DM, TB), BF16), pltpu.VMEM((TB, DM), F32)] + [pltpu.VMEM((TB, 128), F32)] * 2
        + [pltpu.VMEM((TB, 128), jnp.int32), pltpu.SemaphoreType.DMA((2,)), pltpu.SemaphoreType.DMA((1,))],
        compiler_params=pltpu.CompilerParams(vmem_limit_bytes=VMEM_CAP),
    )(g0, g1, g2, w_own, w_oth, z_own, z_oth, lse, msum)


LANES = ((0, 256), (256, 256), (512, 128))


def scatter_kernel(dh, normed, inv_std, gain, lossp, dw_send, dx_out, vec_out, dw_got, *scr):
    bufs = scr[:36]
    vcur, vgot, own_s, ssem, rsem, vssem, vrsem, wsem = scr[36:]
    pos = here()
    barrier_with(ring_peers(pos, (1, 2, 3)))
    wcopy = rcopy(dw_send, dw_got, wsem.at[0], wsem.at[1], shifted(pos, "core", 0))
    wcopy.start()
    half = TOK // 2
    waits = []
    cur = {}

    def view(c, phase, coord, lo):
        lane0, width = LANES[c]
        axis = ORDERS[c][phase]
        rows = pl.ds(lo, half)
        if phase == 0:
            idx = tuple(coord if ax == axis else slice(None) for ax in ("z", "y", "x"))
            return dh.at[idx + (rows, pl.ds(lane0, width))]
        ref, axes = cur[c]
        idx = tuple(coord if ax == axis else slice(None) for ax in axes)
        return ref.at[idx + (rows, slice(None))]

    def add_into(dst, srcs, lead):
        if lead == 0:
            v = dst[...]
            for s in srcs:
                v = v + s[...]
            dst[...] = v
        else:
            def body(j, carry):
                if lead == 1:
                    add_into(dst.at[j], [s.at[j] for s in srcs], 0)
                else:
                    for q in range(SIDE):
                        add_into(dst.at[j, q], [s.at[j, q] for s in srcs], 0)
                return carry
            lax.fori_loop(0, SIDE, body, 0)

    for phase in range(3):
        lead = 2 - phase
        state = []
        for c in range(3):
            axis = ORDERS[c][phase]
            a = pos[axis]
            r1p, r1m, r2p, r2m = bufs[(c * 3 + phase) * 4:(c * 3 + phase) * 4 + 4]
            s0 = (c * 3 + phase) * 6
            pre = (slice(None),) * lead
            right, left = shifted(pos, axis, 1), shifted(pos, axis, -1)
            lo0, lo1 = pre + (pl.ds(0, half), slice(None)), pre + (pl.ds(half, half), slice(None))
            near_r, near_l = (a + 1) % SIDE, (a + SIDE - 1) % SIDE
            far = (a + 2) % SIDE
            sends = [
                rcopy(view(c, phase, far, 0), r1p, ssem.at[s0], rsem.at[s0], right),
                rcopy(view(c, phase, far, half), r1m, ssem.at[s0 + 1], rsem.at[s0 + 1], left),
                rcopy(view(c, phase, near_r, half), r2p.at[lo1], ssem.at[s0 + 2], rsem.at[s0 + 2], right),
                rcopy(view(c, phase, near_l, 0), r2m.at[lo0], ssem.at[s0 + 3], rsem.at[s0 + 3], left),
                rcopy(r1p, r2p.at[lo0], ssem.at[s0 + 4], rsem.at[s0 + 4], right),
                rcopy(r1m, r2m.at[lo1], ssem.at[s0 + 5], rsem.at[s0 + 5], left),
            ]
            for cp in sends[:4]:
                cp.start()
            state.append((sends, r1p, r1m, r2p, r2m, near_r, near_l, a))
        for c in range(3):
            sends, r1p, r1m, r2p, r2m, near_r, near_l, a = state[c]
            sends[0].wait_recv()
            add_into(r1p, [view(c, phase, near_r, 0)], lead)
            sends[4].start()
            sends[1].wait_recv()
            add_into(r1m, [view(c, phase, near_l, half)], lead)
            sends[5].start()
        new = {}
        for c in range(3):
            sends, r1p, r1m, r2p, r2m, near_r, near_l, a = state[c]
            for k in range(2, 6):
                sends[k].wait_recv()
            for lo in (0, half):
                sl = (slice(None),) * lead + (pl.ds(lo, half), slice(None))
                add_into(r2p.at[sl], [r2m.at[sl], view(c, phase, a, lo)], lead)
            axes = tuple(ax for ax in ("z", "y", "x") if ax not in ORDERS[c][:phase + 1])
            new[c] = (r2p, axes)
            waits += sends
        cur.update(new)
    gh = jnp.concatenate([cur[c][0][...] for c in range(3)], axis=1)
    nrm = normed[...]
    dg = jnp.sum(gh * nrm, axis=0, keepdims=True)
    dc = jnp.sum(gh, axis=0, keepdims=True)
    lane_loss = lossp[...]
    for k in range(5):
        own_s[k:k + 1, :] = dg[:, 128 * k:128 * k + 128]
        own_s[5 + k:6 + k, :] = dc[:, 128 * k:128 * k + 128]
    own_s[10:16, :] = jnp.zeros((6, 128), F32)
    own_s[10:11, :] = jnp.sum(lane_loss, axis=0, keepdims=True)
    src = own_s
    slot = 0
    for p, axis in enumerate(("core", "x", "y", "z")):
        deltas = (1,) if axis == "core" else (2, 1, 3)
        cps = []
        for d in deltas:
            cp = rcopy(src, vgot.at[slot], vssem.at[slot], vrsem.at[slot], shifted(pos, axis, d))
            cp.start()
            cps.append((cp, slot))
            slot += 1
        if p == 0:
            q = gh * (1.0 + gain[...])
            cen = q - jnp.mean(q, axis=-1, keepdims=True)
            dx_out[...] = (inv_std[...] * (cen - nrm * jnp.mean(q * nrm, axis=-1, keepdims=True))).astype(BF16)
        for cp, _ in cps:
            cp.wait()
        vals = {d: vgot[s] for d, (_, s) in zip(deltas, cps)}
        if axis == "core":
            tot = src[...] + vals[1]
        else:
            tot = (src[...] + vals[2]) + (vals[1] + vals[3])
        if p < 3:
            vcur[p] = tot
            src = vcur.at[p]
        else:
            vec_out[...] = tot
    for cp in waits:
        cp.wait_send()
    wcopy.wait()


def scatter_call(dh, normed, inv_std, gain, lossp, dw_oth):
    vm = pl.BlockSpec(memory_space=pltpu.VMEM)
    anyspec = pl.BlockSpec(memory_space=pl.ANY)
    half = TOK // 2
    bufs = []
    for c in range(3):
        for phase in range(3):
            lead = (SIDE,) * (2 - phase)
            w = LANES[c][1]
            bufs += [pltpu.VMEM(lead + (half, w), F32)] * 2 + [pltpu.VMEM(lead + (TOK, w), F32)] * 2
    return pl.pallas_call(
        scatter_kernel,
        out_shape=(jax.ShapeDtypeStruct((TOK, DM), BF16), jax.ShapeDtypeStruct((16, 128), F32), jax.ShapeDtypeStruct((DM, VL), F32)),
        in_specs=[vm] * 5 + [anyspec],
        out_specs=(vm, vm, anyspec),
        scratch_shapes=bufs + [pltpu.VMEM((3, 16, 128), F32), pltpu.VMEM((10, 16, 128), F32), pltpu.VMEM((16, 128), F32),
                               pltpu.SemaphoreType.DMA((54,)), pltpu.SemaphoreType.DMA((54,)),
                               pltpu.SemaphoreType.DMA((10,)), pltpu.SemaphoreType.DMA((10,)), pltpu.SemaphoreType.DMA((2,))],
        compiler_params=pltpu.CompilerParams(collective_id=3, has_side_effects=True, vmem_limit_bytes=VMEM_CAP),
    )(dh, normed, inv_std, gain, lossp, dw_oth)


def solution(mesh):
    def per_device(hidden, norm_gain, norm_bias, w_blk, labels, loss_mask):
        x = hidden.reshape(TOK, DM).astype(F32)
        centered = x - jnp.mean(x, axis=-1, keepdims=True)
        inv_std = lax.rsqrt(jnp.mean(centered * centered, axis=-1, keepdims=True) + NORM_EPS)
        normed = centered * inv_std
        h = (normed * (1.0 + norm_gain) + norm_bias).astype(BF16)
        lab = labels.reshape(TOK, 1)
        mask = loss_mask.reshape(TOK, 1)
        lane = lax.broadcasted_iota(jnp.int32, (TOK, 128), 1)
        aux = jnp.where(lane == 0, lab % 256, jnp.where(lane == 1, (lab // 256) % 256, jnp.where(lane == 2, lab // 65536, 0))).astype(F32)
        aux = jnp.where(lane == 3, mask, aux).astype(BF16)
        h2 = jnp.concatenate([h[:, 512:], aux], axis=1)
        g0, g1, g2, w_oth = gather_call(h[:, :256], h[:, 256:512], h2, w_blk)
        g0, g1, g2 = (g.reshape(NTOK, 256) for g in (g0, g1, g2))
        z_own, z_oth, lse_loc, mt, ms = logits_call(g0, g1, g2, w_blk, w_oth)
        lse, msum = lse_call(lse_loc, ms)
        dh, dw_own, dw_oth = grads_call(g0, g1, g2, w_blk, w_oth, z_own, z_oth, lse, msum)
        chip = lax.axis_index("vp") // 2
        own_lse = lax.dynamic_slice(lse.reshape(NTOK), (chip * TOK,), (TOK,))
        loss_lane = jnp.concatenate([mask[:, 0] * own_lse, jnp.zeros((64,), F32)]).reshape(1, 128)
        lossp = jnp.concatenate([-mt, loss_lane, jnp.zeros((7, 128), F32)])
        dx, vec, dw_got = scatter_call(dh.reshape(SIDE, SIDE, SIDE, TOK, DM), normed, jnp.broadcast_to(inv_std, (TOK, DM)),
                                       norm_gain.reshape(1, DM), lossp, dw_oth)
        grad_w = dw_own + dw_got
        loss = jnp.sum(vec[10]) / msum[0, 0]
        return (loss.reshape(1), dx.reshape(hidden.shape), grad_w, vec[0:5].reshape(DM), vec[5:10].reshape(DM))

    tok_spec = P("vp", "dp")
    return jax.shard_map(
        per_device,
        mesh=mesh,
        in_specs=(P("vp", "dp", None), P(None), P(None), P(None, "vp"), tok_spec, tok_spec),
        out_specs=(P("dp"), P("vp", "dp", None), P("dp", "vp"), P("dp"), P("dp")),
        check_vma=False,
    )
```

time: 1110 us -> 308 us (0.28)
  waiting for transfers between devices: 634 us -> 0 us
  Pallas kernels: 0 us -> 279 us
  blocking collectives: 263 us -> 0 us
  matrix products: 133 us -> 0 us
  other arithmetic: 64.5 us -> 16.4 us
  between operations: 16.6 us -> 3.2 us
    reduce_scatter x1 -> x0, waiting for transfers between devices: 633 us -> none  [per_device(): lax.psum_scatter(grad_h_part, 'vp', scatter_dimension=0, tiled=True)]
    pallas_call x0 -> x5, Pallas kernels: none -> 279 us  [the longest x1 89.3 us: grads_call(): pl.pallas_call(grads_kernel, out_shape=(jax.ShapeDtypeStruct((NTOK, DM),...]
    dot_general x3 -> x0, matrix products: 133 us -> none  [the longest x1 55.4 us: per_device(): jnp.einsum('sbv,dv->sbd', grad_logits, w_blk, preferred_element_type=jnp....]
    psum x2 -> x0, blocking collectives: 127 us -> none  [the longest x1 64.3 us: per_device(): sum_exp = lax.psum(jnp.sum(exp_shift, axis=-1), 'vp')]
    all_gather x2 -> x0, blocking collectives: 71.5 us -> none  [the longest x1 37.7 us: per_device(): mask_all = lax.all_gather(loss_mask, 'vp', axis=0, tiled=True)]
    pmax x1 -> x0, blocking collectives: 64.2 us -> none  [per_device(): row_max = lax.pmax(jnp.max(logits, axis=-1), 'vp')]
    convert_element_type x3 -> x1, other arithmetic: 37 us -> 0.1 us  [per_device(): aux = jnp.where(lane == 3, mask, aux).astype(BF16)]
    reduce_sum x6 -> x3, other arithmetic: 26.2 us -> 3.32 us  [the longest x1 1.28 us: per_device(): loss = jnp.sum(vec[10]) / msum[0, 0]]
  transfers between devices with their start and end apart: 2 -> 0, of which waited for: 2 -> 0; matrix products, arithmetic and copies ran while one was open for 4% -> 0% of each run, Pallas kernels for 0% -> 0%
where the time goes in v1:
time: 308 us; the launch traced here: 307 us
  Pallas kernels  279 us (91%)
  other arithmetic  16.4 us (5%)
  local copies, waits for them, and re-layouts  8.61 us (3%)
  between operations  3.2 us (1%)
    pallas_call x1, Pallas kernels, grads_call(): pl.pallas_call(grads_kernel, out_shape=(jax.ShapeDtypeStruct((NTOK, DM),...  89.3 us
    pallas_call x1, Pallas kernels, scatter_call(): pl.pallas_call(scatter_kernel, out_shape=(jax.ShapeDtypeStruct((TOK, DM),...  72.4 us
    pallas_call x1, Pallas kernels, logits_call(): pl.pallas_call(logits_kernel, out_shape=(zshape, zshape, jax.ShapeDtypeSt...  57.2 us
    pallas_call x1, Pallas kernels, gather_call(): pl.pallas_call(gather_kernel, out_shape=(gshape, gshape, gshape, jax.Shap...  45.2 us
    pallas_call x1, Pallas kernels, lse_call(): pl.pallas_call(lse_kernel, out_shape=(jax.ShapeDtypeStruct((NB, TB), F32)...  14.9 us
    add x1, other arithmetic, per_device(): grad_w = dw_own + dw_got  7.93 us

profile of v1, /device:TPU:0, one launch (start us, length us, event | category | flops | bytes accessed | tf_op | source)
XLA Modules:
  0.0 307.3 jit_solution(4299400059780457605)
XLA Ops:
  0.6 1.0 convert_reduce_fusion
  1.6 1.1 multiply_reduce_fusion
  2.7 0.1 rsqrt.12
  2.8 0.0 copy-start.2
  2.8 0.1 div.42
  2.9 0.7 broadcast_add_fusion
  3.6 1.7 fusion
  5.2 0.6 fusion.2
  5.8 0.8 reshape.237
  6.6 0.8 broadcast_in_dim.44
  7.4 0.0 copy-start.3
  7.4 0.1 select_convert_fusion
  7.5 0.0 copy-done.2
  7.5 0.4 copy-done.3
  7.9 0.6 pad_maximum_fusion.h2
  8.5 45.2 %shard_map.101 = (bf16[4,4,4,64,256]{4,3,2,1,0:T(8,128)(2,1)}, bf16[4,4,4,64,256]{4,3,2,1,0:T(8,128)(2,1)}, bf16[4,4,4,64,256]{4,3,2,1,0:T(8,128)(2,1)}, bf16[640,2048]{1,0:T(8,128)(2,1)}) custom-call(bf16[64,256]{1,0:T(8,128)(2,1)} %get-tuple-element.42.h0, bf16[64,256]{1,0:T(8,128)(2,1)} %get-tuple-element.41.h1, bf16[64,256]{1,0:T(8,128)(2,1)} %pad_maximum_fusion.h2, ...), custom_call_target="tpu_custom_call" | custom-call | tf_op jit(solution)/shard_map/pallas_call | solution.py:124
  53.7 57.2 %shard_map.102 = (f32[4096,2048]{1,0:T(8,128)}, f32[4096,2048]{1,0:T(8,128)}, f32[8,512]{1,0:T(8,128)}, f32[8,128]{1,0:T(8,128)}, f32[8,128]{1,0:T(8,128)}) custom-call(bf16[4096,256]{1,0:T(8,128)(2,1)} %bitcast.22, bf16[4096,256]{1,0:T(8,128)(2,1)} %bitcast.24, bf16[4096,256]{1,0:T(8,128)(2,1)} %bitcast.26, bf16[640,2048]{1,0:T(8,128)(2,1)} %w_own.3, ...), custom_call_target="tpu_custom_call" | custom-call | tf_op jit(solution)/shard_map/pallas_call | solution.py:228
  111.0 14.9 %shard_map.103 = (f32[8,512]{1,0:T(8,128)}, f32[8,128]{1,0:T(8,128)}) custom-call(f32[8,512]{1,0:T(8,128)} %get-tuple-element.28.lse_in, f32[8,128]{1,0:T(8,128)} %get-tuple-element.29.ms_in), custom_call_target="tpu_custom_call" | custom-call | tf_op jit(solution)/shard_map/pallas_call | solution.py:269
  125.9 89.3 %shard_map.104 = (f32[4096,640]{1,0:T(8,128)}, f32[640,2048]{1,0:T(8,128)}, f32[640,2048]{1,0:T(8,128)}) custom-call(bf16[4096,256]{1,0:T(8,128)(2,1)} %bitcast.23, bf16[4096,256]{1,0:T(8,128)(2,1)} %bitcast.25, bf16[4096,256]{1,0:T(8,128)(2,1)} %bitcast.27, bf16[640,2048]{1,0:T(8,128)(2,1)} %w_own.3, bf16[640,2048]{1,0:T(8,128)(2,1)} %get-tuple-element.25.w_oth, ...), custom_call_target="tpu_custom_call" | custom-call | tf_op jit(solution)/shard_map/pallas_call | solution.py:376
  215.2 1.4 mul.27.inv_std
  216.6 1.3 reshape.242.gain
  217.9 0.7 copy.11
  218.6 0.7 dynamic-slice_multiply_fusion
  219.3 0.7 neg.3
  220.0 0.1 pad.3.clone
  220.1 0.7 maximum_maximum_fusion.lossp
  220.7 72.4 %shard_map.105 = (bf16[64,640]{1,0:T(8,128)(2,1)}, f32[16,128]{1,0:T(8,128)}, f32[640,2048]{1,0:T(8,128)}) custom-call(f32[4,4,4,64,640]{4,3,2,1,0:T(8,128)} %bitcast.21, f32[64,640]{1,0:T(8,128)} %get-tuple-element.39.normed, f32[64,640]{1,0:T(8,128)} %mul.27.inv_std, f32[1,640]{1,0:T(1,128)} %reshape.242.gain, f32[16,128]{1,0:T(8,128)} %maximum_maximum_fusion.lossp, ...), custom_call_target="tpu_custom_call" | custom-call | tf_op jit(solution)/shard_map/pallas_call | solution.py:524
  293.1 1.3 slice_reduce_fusion
  294.4 1.2 slice.25
  296.9 0.0 copy-start.1
  296.9 0.0 copy-start
  296.9 7.9 %add.76 = f32[640,2048]{1,0:T(8,128)} add(f32[640,2048]{1,0:T(8,128)} %get-tuple-element.37, f32[640,2048]{1,0:T(8,128)} %get-tuple-element.38) | non-fusion elementwise | flops 1310720 | bytes 15728640 | tf_op jit(solution)/shard_map/add | solution.py:560
  304.9 0.0 copy-done.1
  304.9 0.6 slice_bitcast_fusion
  305.5 0.0 copy-done
  305.5 0.6 copy.13
  (8 shorter events, 0.1 us)
Async XLA Ops:
  2.8 4.7 %copy-start.2 = (f32[64]{0:T(128)}, f32[64]{0:T(128)S(1)}, u32[]{:S(2)}) copy-start(f32[64]{0:T(128)S(1)} %rsqrt.12) | copy-start | bytes 772
  7.4 0.5 copy-start.3
  296.9 8.0 %copy-start.1 = (f32[16,128]{1,0:T(8,128)S(1)}, f32[16,128]{1,0:T(8,128)}, u32[]{:S(2)}) copy-start(f32[16,128]{1,0:T(8,128)} %get-tuple-element.35) | copy-start | bytes 24580
  296.9 8.5 %copy-start = (bf16[64,640]{1,0:T(8,128)(2,1)S(1)}, bf16[64,640]{1,0:T(8,128)(2,1)}, u32[]{:S(2)}) copy-start(bf16[64,640]{1,0:T(8,128)(2,1)} %get-tuple-element.36) | copy-start | bytes 245764

commit v2 on v1

--- a/solution.py
+++ b/solution.py
@@ -18,6 +18,7 @@
 TB = 512
 NB = NTOK // TB
 CT = 1024
+NSEG = 2 * VL // CT
 VMEM_CAP = 64 * 1024 * 1024 - 65536
 
 
@@ -105,7 +106,7 @@
                 slot = (c * 3 + phase) * 4 + 2 + k
                 first[c, k].wait_recv()
                 blk = gs[c].at[unit(c, phase, (me - d + SIDE) % SIDE)]
-                half = blk.at[(slice(None),) * (phase + 1) + (pl.ds(128 * k, 128),)]
+                half = blk.at[(slice(None),) * phase + (k,)]
                 cp = rcopy(half, half, ssem.at[slot], rsem.at[slot], shifted(pos, axis, d))
                 cp.start()
                 sends.append(cp)
@@ -120,7 +121,7 @@
 def gather_call(h0, h1, h2, w_blk):
     vm = pl.BlockSpec(memory_space=pltpu.VMEM)
     anyspec = pl.BlockSpec(memory_space=pl.ANY)
-    gshape = jax.ShapeDtypeStruct((SIDE, SIDE, SIDE, TOK, 256), BF16)
+    gshape = jax.ShapeDtypeStruct((SIDE, SIDE, SIDE, 2, TOK, 128), BF16)
     return pl.pallas_call(
         gather_kernel,
         out_shape=(gshape, gshape, gshape, jax.ShapeDtypeStruct((DM, VL), BF16)),
@@ -138,36 +139,55 @@
     return lab.astype(jnp.int32) - lane
 
 
-def logits_kernel(g0, g1, g2, w_own, w_oth, z_own, z_oth, lse_out, mt_out, ms_out,
-                  zA, zB, m_s, s_s, t_s, lab_s, sem):
+def tok_tile(g_ref, i, k):
+    return g_ref[pl.ds(i * (TB // TOK), TB // TOK), k].reshape(TB, 128)
+
+
+def load_w(w_own, w_oth, wt, wsem):
+    cps = []
+    for half, ref in enumerate((w_own, w_oth)):
+        for k in range(VL // 128):
+            cp = pltpu.make_async_copy(ref.at[:, pl.ds(128 * k, 128)], wt.at[half * (VL // 128) + k], wsem.at[half * (VL // 128) + k])
+            cp.start()
+            cps.append(cp)
+    for cp in cps:
+        cp.wait()
+
+
+def w_pair(wt, j, lo, hi):
+    return jnp.concatenate([wt[2 * j, lo:hi, :], wt[2 * j + 1, lo:hi, :]], axis=1)
+
+
+def logits_kernel(g0, g1, g2, w_own, w_oth, z_out, lse_out, mt_out, ms_out,
+                  zb, wt, m_s, s_s, t_s, lab_s, sem, wsem):
     pos = here()
     base_own = dev_of(pos) * VL
     base_oth = dev_of({**pos, "core": 1 - pos["core"]}) * VL
-    zbuf = (zA, zB)
-    tiles = ((w_own, z_own, 0, base_own), (w_own, z_own, CT, base_own), (w_oth, z_oth, 0, base_oth), (w_oth, z_oth, CT, base_oth))
+    load_w(w_own, w_oth, wt, wsem)
     mt_out[...] = jnp.zeros_like(mt_out)
     ms_out[...] = jnp.zeros_like(ms_out)
 
-    def stats(buf, cbase, first, rows):
-        zt = buf[rows, :]
-        tile_max = zt[:, 0:128]
-        for k in range(1, CT // 128):
-            tile_max = jnp.maximum(tile_max, zt[:, 128 * k:128 * k + 128])
+    def stats(buf, seg, cbase, rows):
+        c0 = seg * CT
+        nk = CT // 128
+        tile_max = buf[rows, pl.ds(c0, 128)]
+        for k in range(1, nk):
+            tile_max = jnp.maximum(tile_max, buf[rows, pl.ds(c0 + 128 * k, 128)])
         labm = lab_s[rows, :]
-        if first:
+        if seg == 0:
             m_new = tile_max
         else:
             m_old = m_s[rows, :]
             m_new = jnp.maximum(m_old, tile_max)
         acc = None
         tacc = None
-        for k in range(CT // 128):
-            zk = zt[:, 128 * k:128 * k + 128]
+        for k in range(nk):
+            zk = buf[rows, pl.ds(c0 + 128 * k, 128)]
             e = jnp.exp(zk - m_new)
             hit = jnp.where(labm == cbase + 128 * k, zk, 0.0)
             acc = e if acc is None else acc + e
             tacc = hit if tacc is None else tacc + hit
-        if first:
+        if seg == 0:
             s_s[rows, :] = acc
             t_s[rows, :] = tacc
         else:
@@ -175,37 +195,34 @@
             t_s[rows, :] = t_s[rows, :] + tacc
         m_s[rows, :] = m_new
 
+    def zcopy(i):
+        return pltpu.make_async_copy(zb.at[i % 2], z_out.at[pl.ds(pl.multiple_of(i * TB, TB), TB), :], sem.at[i % 2])
+
     def block(i, carry):
-        tok = pl.ds(pl.multiple_of(i * TB, TB), TB)
-        a0 = g0[tok, :]
-        a1 = g1[tok, :]
-        a2 = g2[tok, 0:128]
-        aux = g2[tok, 128:256].astype(F32)
+        @pl.when(i >= 2)
+        def _():
+            zcopy(i - 2).wait()
+        buf = zb.at[i % 2]
+        a0 = jnp.concatenate([tok_tile(g0, i, 0), tok_tile(g0, i, 1)], axis=1)
+        a1 = jnp.concatenate([tok_tile(g1, i, 0), tok_tile(g1, i, 1)], axis=1)
+        a2 = tok_tile(g2, i, 0)
+        aux = tok_tile(g2, i, 1).astype(F32)
         lab_s[...] = label_minus_lane(aux)
-        for seg in range(5):
-            if seg < 4:
-                w_ref, z_ref, off, _ = tiles[seg]
-                buf = zbuf[seg % 2]
-                out = pltpu.make_async_copy(buf, z_ref.at[tok, pl.ds(off, CT)], sem.at[seg % 2])
-                if seg >= 2:
-                    out.wait()
-                else:
-                    @pl.when(i > 0)
-                    def _():
-                        out.wait()
-            for sub in range(4):
-                if seg < 4:
-                    cols = pl.ds(off + 256 * sub, 256)
-                    zt = jnp.dot(a0, w_ref[0:256, cols], preferred_element_type=F32)
-                    zt += jnp.dot(a1, w_ref[256:512, cols], preferred_element_type=F32)
-                    zt += jnp.dot(a2, w_ref[512:640, cols], preferred_element_type=F32)
-                    buf[:, 256 * sub:256 * sub + 256] = zt
+        nsub = CT // 256
+        nrow = TB // 16 // nsub
+        for seg in range(NSEG + 1):
+            for sub in range(nsub):
+                if seg < NSEG:
+                    j = seg * nsub + sub
+                    zt = jnp.dot(a0, w_pair(wt, j, 0, 256), preferred_element_type=F32)
+                    zt += jnp.dot(a1, w_pair(wt, j, 256, 512), preferred_element_type=F32)
+                    zt += jnp.dot(a2, w_pair(wt, j, 512, 640), preferred_element_type=F32)
+                    buf[:, 256 * j:256 * j + 256] = zt
                 if seg > 0:
-                    _, _, poff, pbase = tiles[seg - 1]
-                    for r in range(8):
-                        stats(zbuf[(seg - 1) % 2], pbase + poff, seg == 1, pl.ds(sub * 128 + r * 16, 16))
-            if seg < 4:
-                out.start()
+                    half = (seg - 1) // (NSEG // 2)
+                    cbase = (base_own, base_oth)[half] + ((seg - 1) % (NSEG // 2)) * CT
+                    for r in range(nrow):
+                        stats(buf, seg - 1, cbase, pl.ds((sub * nrow + r) * 16, 16))
         mt = m_s[...].T
         st = s_s[...].T
         mx = jnp.max(mt, axis=0, keepdims=True)
@@ -214,24 +231,24 @@
         mcol = aux[:, 3:4]
         mt_out[...] += jnp.sum((t_s[...] * mcol).reshape(TB // 8, 8, 128), axis=0)
         ms_out[...] += jnp.sum(jnp.broadcast_to(mcol, (TB, 128)).reshape(TB // 8, 8, 128), axis=0)
+        zcopy(i).start()
         return carry
 
     lax.fori_loop(0, NB, block, 0)
-    for k in range(2):
-        pltpu.make_async_copy(zbuf[k], z_oth.at[pl.ds(0, TB), pl.ds(0, CT)], sem.at[k]).wait()
+    zcopy(NB - 2).wait()
+    zcopy(NB - 1).wait()
 
 
 def logits_call(g0, g1, g2, w_own, w_oth):
     vm = pl.BlockSpec(memory_space=pltpu.VMEM)
     anyspec = pl.BlockSpec(memory_space=pl.ANY)
-    zshape = jax.ShapeDtypeStruct((NTOK, VL), F32)
     return pl.pallas_call(
         logits_kernel,
-        out_shape=(zshape, zshape, jax.ShapeDtypeStruct((NB, TB), F32), jax.ShapeDtypeStruct((8, 128), F32), jax.ShapeDtypeStruct((8, 128), F32)),
-        in_specs=[vm] * 5,
-        out_specs=(anyspec, anyspec, vm, vm, vm),
-        scratch_shapes=[pltpu.VMEM((TB, CT), F32), pltpu.VMEM((TB, CT), F32)] + [pltpu.VMEM((TB, 128), F32)] * 3
-        + [pltpu.VMEM((TB, 128), jnp.int32), pltpu.SemaphoreType.DMA((2,))],
+        out_shape=(jax.ShapeDtypeStruct((NTOK, 2 * VL), F32), jax.ShapeDtypeStruct((NB, TB), F32), jax.ShapeDtypeStruct((8, 128), F32), jax.ShapeDtypeStruct((8, 128), F32)),
+        in_specs=[vm] * 3 + [anyspec] * 2,
+        out_specs=(anyspec, vm, vm, vm),
+        scratch_shapes=[pltpu.VMEM((2, TB, 2 * VL), F32), pltpu.VMEM((2 * VL // 128, DM, 128), BF16)] + [pltpu.VMEM((TB, 128), F32)] * 3
+        + [pltpu.VMEM((TB, 128), jnp.int32), pltpu.SemaphoreType.DMA((2,)), pltpu.SemaphoreType.DMA((2 * VL // 128,))],
         compiler_params=pltpu.CompilerParams(vmem_limit_bytes=VMEM_CAP),
     )(g0, g1, g2, w_own, w_oth)
 
@@ -277,112 +294,112 @@
     )(lse_loc, msum)
 
 
-def grads_kernel(g0, g1, g2, w_own, w_oth, z_own, z_oth, lse, msum, dh_out, dw_own, dw_oth,
-                 zA, zB, dA, dB, hT, dh_s, lse_s, wt_s, lab_s, zsem, osem):
+def grads_kernel(g0, g1, g2, w_own, w_oth, z_in, lse, msum, dh_out, dw_own, dw_oth,
+                 zb, db, wt, hT, dh_s, lse_s, wt_s, lab_s, zsem, osem, wsem):
     pos = here()
     base_own = dev_of(pos) * VL
     base_oth = dev_of({**pos, "core": 1 - pos["core"]}) * VL
-    zbuf, dbuf = (zA, zB), (dA, dB)
-    tiles = ((w_own, z_own, 0, base_own, dw_own), (w_own, z_own, CT, base_own, dw_own),
-             (w_oth, z_oth, 0, base_oth, dw_oth), (w_oth, z_oth, CT, base_oth, dw_oth))
-
-    def zcopy(i, t):
-        _, z_ref, off, _, _ = tiles[t]
-        tok = pl.ds(pl.multiple_of(i * TB, TB), TB)
-        return pltpu.make_async_copy(z_ref.at[tok, pl.ds(off, CT)], zbuf[t % 2], zsem.at[t % 2])
-
-    def prep(i):
-        tok = pl.ds(pl.multiple_of(i * TB, TB), TB)
-        aux = g2[tok, 128:256].astype(F32)
+
+    def zcopy(i):
+        return pltpu.make_async_copy(z_in.at[pl.ds(pl.multiple_of(i * TB, TB), TB), :], zb.at[i % 2], zsem.at[i % 2])
+
+    def ocopy(i):
+        return pltpu.make_async_copy(dh_s.at[i % 2], dh_out.at[pl.ds(pl.multiple_of(i * TB, TB), TB), :], osem.at[i % 2])
+
+    zcopy(0).start()
+    zcopy(1).start()
+    dw_own[...] = jnp.zeros_like(dw_own)
+    dw_oth[...] = jnp.zeros_like(dw_oth)
+    load_w(w_own, w_oth, wt, wsem)
+    nsub = CT // 256
+
+    def block(i, carry):
+        zcopy(i).wait()
+
+        @pl.when(i >= 2)
+        def _():
+            ocopy(i - 2).wait()
+        zbuf = zb.at[i % 2]
+        dhb = dh_s.at[i % 2]
+        aux = tok_tile(g2, i, 1).astype(F32)
         lab_s[...] = label_minus_lane(aux)
         wt_s[...] = jnp.broadcast_to(aux[:, 3:4], (TB, 128)) / msum[0:1, :]
         lse_s[...] = jnp.broadcast_to(lse[pl.ds(i, 1), :], (128, TB)).T
-
-    def make_dz(t, r):
-        _, _, off, base, _ = tiles[t]
-        rows = pl.ds(r * 16, 16)
-        lse_b = lse_s[rows, :]
-        wt = wt_s[rows, :]
-        labm = lab_s[rows, :]
-        for k in range(CT // 128):
-            ks = slice(128 * k, 128 * k + 128)
-            p = jnp.exp(zbuf[t % 2][rows, ks] - lse_b)
-            p = jnp.where(labm == base + off + 128 * k, p - 1.0, p)
-            dbuf[t % 2][rows, ks] = (p * wt).astype(BF16)
-
-    dw_own[...] = jnp.zeros_like(dw_own)
-    dw_oth[...] = jnp.zeros_like(dw_oth)
-    zcopy(0, 0).start()
-    zcopy(0, 1).start()
-    prep(0)
-    zcopy(0, 0).wait()
-    for r in range(TB // 16):
-        make_dz(0, r)
-    zcopy(0, 2).start()
-
-    def block(i, carry):
-        tok = pl.ds(pl.multiple_of(i * TB, TB), TB)
-        hT[0:256, :] = g0[tok, :].T
-        hT[256:512, :] = g1[tok, :].T
-        hT[512:640, :] = g2[tok, 0:128].T
-        for seg in range(4):
-            w_ref, _, off, _, dw_ref = tiles[seg]
-            dz = dbuf[seg % 2]
-            nt = (seg + 1) % 4
-            if seg == 3:
-                nxt = jnp.minimum(i + 1, NB - 1)
-                prep(nxt)
-            else:
-                nxt = i
-            zcopy(nxt, nt).wait()
+        for k, g in enumerate((g0, g1, g2)):
+            hT[256 * k:256 * k + 128, :] = tok_tile(g, i, 0).T
+            if k < 2:
+                hT[256 * k + 128:256 * k + 256, :] = tok_tile(g, i, 1).T
+
+        def make_dz(seg, r):
+            half = seg // (NSEG // 2)
+            base = (base_own, base_oth)[half] + (seg % (NSEG // 2)) * CT
+            rows = pl.ds(r * 16, 16)
+            lse_b = lse_s[rows, :]
+            w_b = wt_s[rows, :]
+            labm = lab_s[rows, :]
+            for k in range(CT // 128):
+                p = jnp.exp(zbuf[rows, pl.ds(seg * CT + 128 * k, 128)] - lse_b)
+                p = jnp.where(labm == base + 128 * k, p - 1.0, p)
+                db[seg * (CT // 128) + k, rows, :] = (p * w_b).astype(BF16)
+
+        for r in range(TB // 16):
+            make_dz(0, r)
+        for seg in range(NSEG):
             piece = 0
+            dz = [jnp.concatenate([db[2 * j], db[2 * j + 1]], axis=1) for j in range(seg * nsub, seg * nsub + nsub)]
+            ops = []
             for n in range(3):
-                lo, hi = 256 * n, min(256 * n + 256, DM)
-                part = lax.dot_general(dz[...], w_ref[lo:hi, pl.ds(off, CT)], (((1,), (1,)), ((), ())), preferred_element_type=F32)
-                if seg == 0:
-                    dh_s[:, lo:hi] = part
+                ops.append(("h", n))
+            for sub in range(nsub):
+                ops.append(("w", sub))
+            per = -(-(TB // 16) // len(ops))
+            for kind, n in ops:
+                if kind == "h":
+                    lo, hi = 256 * n, min(256 * n + 256, DM)
+                    part = None
+                    for sub in range(nsub):
+                        q = lax.dot_general(dz[sub], w_pair(wt, seg * nsub + sub, lo, hi), (((1,), (1,)), ((), ())), preferred_element_type=F32)
+                        part = q if part is None else part + q
+                    if seg == 0:
+                        dhb[:, lo:hi] = part
+                    else:
+                        dhb[:, lo:hi] += part
                 else:
-                    dh_s[:, lo:hi] += part
-                for r in range(4):
-                    make_dz(nt, piece)
-                    piece += 1
-            for sub in range(4):
-                cols = pl.ds(off + 256 * sub, 256)
-                dw_ref[:, cols] += jnp.dot(hT[...], dz[:, 256 * sub:256 * sub + 256], preferred_element_type=F32)
-                for r in range(5):
-                    make_dz(nt, piece)
-                    piece += 1
-            after = jnp.minimum(i + (seg + 3) // 4, NB - 1)
-            zcopy(after, (seg + 3) % 4).start()
+                    half = seg // (NSEG // 2)
+                    off = (seg % (NSEG // 2)) * CT + 256 * n
+                    dw_ref = (dw_own, dw_oth)[half]
+                    dw_ref[:, off:off + 256] += jnp.dot(hT[...], dz[n], preferred_element_type=F32)
+                if seg + 1 < NSEG:
+                    for r in range(per):
+                        if piece < TB // 16:
+                            make_dz(seg + 1, piece)
+                            piece += 1
+        ocopy(i).start()
+
+        @pl.when(i + 2 < NB)
+        def _():
+            zcopy(i + 2).start()
         return carry
 
-    def block_out(i, carry):
-        block(i, carry)
-        tok = pl.ds(pl.multiple_of(i * TB, TB), TB)
-        cp = pltpu.make_async_copy(dh_s, dh_out.at[tok, :], osem.at[0])
-        cp.start()
-        cp.wait()
-        return carry
-
-    lax.fori_loop(0, NB, block_out, 0)
-    zcopy(NB - 1, 1).wait()
-    zcopy(NB - 1, 2).wait()
-
-
-def grads_call(g0, g1, g2, w_own, w_oth, z_own, z_oth, lse, msum):
+    lax.fori_loop(0, NB, block, 0)
+    ocopy(NB - 2).wait()
+    ocopy(NB - 1).wait()
+
+
+def grads_call(g0, g1, g2, w_own, w_oth, z, lse, msum):
     vm = pl.BlockSpec(memory_space=pltpu.VMEM)
     anyspec = pl.BlockSpec(memory_space=pl.ANY)
     dwshape = jax.ShapeDtypeStruct((DM, VL), F32)
     return pl.pallas_call(
         grads_kernel,
         out_shape=(jax.ShapeDtypeStruct((NTOK, DM), F32), dwshape, dwshape),
-        in_specs=[vm] * 5 + [anyspec] * 2 + [vm] * 2,
+        in_specs=[vm] * 3 + [anyspec] * 3 + [vm] * 2,
         out_specs=(anyspec, vm, vm),
-        scratch_shapes=[pltpu.VMEM((TB, CT), F32)] * 2 + [pltpu.VMEM((TB, CT), BF16)] * 2
-        + [pltpu.VMEM((DM, TB), BF16), pltpu.VMEM((TB, DM), F32)] + [pltpu.VMEM((TB, 128), F32)] * 2
-        + [pltpu.VMEM((TB, 128), jnp.int32), pltpu.SemaphoreType.DMA((2,)), pltpu.SemaphoreType.DMA((1,))],
+        scratch_shapes=[pltpu.VMEM((2, TB, 2 * VL), F32), pltpu.VMEM((2 * VL // 128, TB, 128), BF16), pltpu.VMEM((2 * VL // 128, DM, 128), BF16),
+                        pltpu.VMEM((DM, TB), BF16), pltpu.VMEM((2, TB, DM), F32)] + [pltpu.VMEM((TB, 128), F32)] * 2
+        + [pltpu.VMEM((TB, 128), jnp.int32), pltpu.SemaphoreType.DMA((2,)), pltpu.SemaphoreType.DMA((2,)), pltpu.SemaphoreType.DMA((2 * VL // 128,))],
         compiler_params=pltpu.CompilerParams(vmem_limit_bytes=VMEM_CAP),
-    )(g0, g1, g2, w_own, w_oth, z_own, z_oth, lse, msum)
+    )(g0, g1, g2, w_own, w_oth, z, lse, msum)
 
 
 LANES = ((0, 256), (256, 256), (512, 128))
@@ -545,12 +562,12 @@
         lane = lax.broadcasted_iota(jnp.int32, (TOK, 128), 1)
         aux = jnp.where(lane == 0, lab % 256, jnp.where(lane == 1, (lab // 256) % 256, jnp.where(lane == 2, lab // 65536, 0))).astype(F32)
         aux = jnp.where(lane == 3, mask, aux).astype(BF16)
-        h2 = jnp.concatenate([h[:, 512:], aux], axis=1)
-        g0, g1, g2, w_oth = gather_call(h[:, :256], h[:, 256:512], h2, w_blk)
-        g0, g1, g2 = (g.reshape(NTOK, 256) for g in (g0, g1, g2))
-        z_own, z_oth, lse_loc, mt, ms = logits_call(g0, g1, g2, w_blk, w_oth)
+        parts = [jnp.stack([h[:, 0:128], h[:, 128:256]]), jnp.stack([h[:, 256:384], h[:, 384:512]]), jnp.stack([h[:, 512:], aux])]
+        g0, g1, g2, w_oth = gather_call(*parts, w_blk)
+        g0, g1, g2 = (g.reshape(NTOK // TOK, 2, TOK, 128) for g in (g0, g1, g2))
+        z, lse_loc, mt, ms = logits_call(g0, g1, g2, w_blk, w_oth)
         lse, msum = lse_call(lse_loc, ms)
-        dh, dw_own, dw_oth = grads_call(g0, g1, g2, w_blk, w_oth, z_own, z_oth, lse, msum)
+        dh, dw_own, dw_oth = grads_call(g0, g1, g2, w_blk, w_oth, z, lse, msum)
         chip = lax.axis_index("vp") // 2
         own_lse = lax.dynamic_slice(lse.reshape(NTOK), (chip * TOK,), (TOK,))
         loss_lane = jnp.concatenate([mask[:, 0] * own_lse, jnp.zeros((64,), F32)]).reshape(1, 128)

time: 308 us -> 273 us (0.89)
  Pallas kernels: 279 us -> 244 us
    pallas_call x1, Pallas kernels: 89.3 us -> 70 us  [grads_call(): pl.pallas_call(grads_kernel, out_shape=(jax.ShapeDtypeStruct((NTOK, DM),...]
    pallas_call x1, Pallas kernels: 57.2 us -> 41.8 us  [logits_call(): pl.pallas_call(logits_kernel, out_shape=(jax.ShapeDtypeStruct((NTOK, 2 *...]
where the time goes in v2:
time: 273 us
  Pallas kernels  244 us (89%)
  other arithmetic  17.1 us (6%)
  local copies, waits for them, and re-layouts  8.17 us (3%)
  between operations  3.19 us (1%)
    pallas_call x1, Pallas kernels, scatter_call(): pl.pallas_call(scatter_kernel, out_shape=(jax.ShapeDtypeStruct((TOK, DM),...  72.4 us
    pallas_call x1, Pallas kernels, grads_call(): pl.pallas_call(grads_kernel, out_shape=(jax.ShapeDtypeStruct((NTOK, DM),...  70 us
    pallas_call x1, Pallas kernels, gather_call(): pl.pallas_call(gather_kernel, out_shape=(gshape, gshape, gshape, jax.Shap...  45.2 us
    pallas_call x1, Pallas kernels, logits_call(): pl.pallas_call(logits_kernel, out_shape=(jax.ShapeDtypeStruct((NTOK, 2 *...  41.8 us
    pallas_call x1, Pallas kernels, lse_call(): pl.pallas_call(lse_kernel, out_shape=(jax.ShapeDtypeStruct((NB, TB), F32)...  14.9 us
    add x1, other arithmetic, per_device(): grad_w = dw_own + dw_got  7.93 us

profile of v2, /device:TPU:0, one launch (start us, length us, event | category | flops | bytes accessed | tf_op | source)
XLA Modules:
  0.0 272.7 jit_solution(18390119693295210967)
XLA Ops:
  0.6 1.0 convert_reduce_fusion
  1.6 1.1 multiply_reduce_fusion
  2.7 0.1 rsqrt.12
  2.8 0.0 copy-start.2
  2.8 0.1 div.42
  2.9 0.7 broadcast_add_fusion
  3.6 1.6 fusion
  5.2 0.0 copy-done.2
  5.2 0.6 pad_maximum_fusion
  5.8 0.8 reshape.420
  6.6 0.8 broadcast_in_dim.44
  7.4 0.0 copy-start.3
  7.4 0.6 copy-done.3
  8.0 0.1 select_convert_fusion
  8.1 0.6 pad_maximum_fusion.2.h2
  8.7 45.2 %shard_map.101 = (bf16[4,4,4,2,64,128]{5,4,3,2,1,0:T(8,128)(2,1)}, bf16[4,4,4,2,64,128]{5,4,3,2,1,0:T(8,128)(2,1)}, bf16[4,4,4,2,64,128]{5,4,3,2,1,0:T(8,128)(2,1)}, bf16[640,2048]{1,0:T(8,128)(2,1)}) custom-call(bf16[2,64,128]{2,1,0:T(8,128)(2,1)} %get-tuple-element.49.h0, bf16[2,64,128]{2,1,0:T(8,128)(2,1)} %get-tuple-element.50.h1, ...), custom_call_target="tpu_custom_call" | custom-call | tf_op jit(solution)/shard_map/pallas_call | solution.py:125
  53.9 41.8 %shard_map.102 = (f32[4096,4096]{1,0:T(8,128)}, f32[8,512]{1,0:T(8,128)}, f32[8,128]{1,0:T(8,128)}, f32[8,128]{1,0:T(8,128)}) custom-call(bf16[64,2,64,128]{3,2,1,0:T(8,128)(2,1)} %bitcast.32, bf16[64,2,64,128]{3,2,1,0:T(8,128)(2,1)} %bitcast.34, bf16[64,2,64,128]{3,2,1,0:T(8,128)(2,1)} %bitcast.36, bf16[640,2048]{1,0:T(8,128)(2,1)} %w_own.3, ...), custom_call_target="tpu_custom_call" | custom-call | tf_op jit(solution)/shard_map/pallas_call | solution.py:245
  95.6 14.9 %shard_map.103 = (f32[8,512]{1,0:T(8,128)}, f32[8,128]{1,0:T(8,128)}) custom-call(f32[8,512]{1,0:T(8,128)} %get-tuple-element.26.lse_in, f32[8,128]{1,0:T(8,128)} %get-tuple-element.27.ms_in), custom_call_target="tpu_custom_call" | custom-call | tf_op jit(solution)/shard_map/pallas_call | solution.py:286
  110.5 70.0 %shard_map.104 = (f32[4096,640]{1,0:T(8,128)}, f32[640,2048]{1,0:T(8,128)}, f32[640,2048]{1,0:T(8,128)}) custom-call(bf16[64,2,64,128]{3,2,1,0:T(8,128)(2,1)} %bitcast.33, bf16[64,2,64,128]{3,2,1,0:T(8,128)(2,1)} %bitcast.35, bf16[64,2,64,128]{3,2,1,0:T(8,128)(2,1)} %bitcast.37, bf16[640,2048]{1,0:T(8,128)(2,1)} %w_own.3, ...), custom_call_target="tpu_custom_call" | custom-call | tf_op jit(solution)/shard_map/pallas_call | solution.py:393
  180.6 1.4 mul.27.inv_std
  182.0 1.3 reshape.425.gain
  183.2 0.7 copy.11
  184.0 0.7 dynamic-slice_multiply_fusion
  184.7 0.7 neg.3
  185.4 0.1 pad.3.clone
  185.5 0.7 maximum_maximum_fusion.lossp
  186.2 72.4 %shard_map.105 = (bf16[64,640]{1,0:T(8,128)(2,1)}, f32[16,128]{1,0:T(8,128)}, f32[640,2048]{1,0:T(8,128)}) custom-call(f32[4,4,4,64,640]{4,3,2,1,0:T(8,128)} %bitcast.31, f32[64,640]{1,0:T(8,128)} %get-tuple-element.37.normed, f32[64,640]{1,0:T(8,128)} %mul.27.inv_std, f32[1,640]{1,0:T(1,128)} %reshape.425.gain, f32[16,128]{1,0:T(8,128)} %maximum_maximum_fusion.lossp, ...), custom_call_target="tpu_custom_call" | custom-call | tf_op jit(solution)/shard_map/pallas_call | solution.py:541
  258.6 1.3 slice_reduce_fusion
  259.8 1.2 slice.33
  262.4 0.0 copy-start.1
  262.4 0.0 copy-start
  262.4 7.9 %add.76 = f32[640,2048]{1,0:T(8,128)} add(f32[640,2048]{1,0:T(8,128)} %get-tuple-element.35, f32[640,2048]{1,0:T(8,128)} %get-tuple-element.36) | non-fusion elementwise | flops 1310720 | bytes 15728640 | tf_op jit(solution)/shard_map/add | solution.py:577
  270.3 0.0 copy-done.1
  270.3 0.6 slice_bitcast_fusion.5
  270.9 0.0 copy-done
  270.9 0.6 copy.13
  (8 shorter events, 0.1 us)
Async XLA Ops:
  2.8 2.4 copy-start.2
  7.4 0.6 copy-start.3
  262.4 8.0 %copy-start.1 = (f32[16,128]{1,0:T(8,128)S(1)}, f32[16,128]{1,0:T(8,128)}, u32[]{:S(2)}) copy-start(f32[16,128]{1,0:T(8,128)} %get-tuple-element.33) | copy-start | bytes 24580
  262.4 8.5 %copy-start = (bf16[64,640]{1,0:T(8,128)(2,1)S(1)}, bf16[64,640]{1,0:T(8,128)(2,1)}, u32[]{:S(2)}) copy-start(bf16[64,640]{1,0:T(8,128)(2,1)} %get-tuple-element.34) | copy-start | bytes 245764
